TPU v7x, 32 devices: a whole 2x2x4 slice. The times are simulated.
32 devices in a mesh: bank: 4 (over z), zero: 8 (over y, x, core).
Axes of the slice: x: 2, y: 2, z: 4, core: 2. Of those that a mesh axis runs over, the one named last changes fastest.
Arguments:
- master_gate: float32 [64, 2048, 1024], P('bank', 'zero'), may hold values from -0.1875 to 0.1875
- second_gate: bfloat16 [64, 2048, 1024], P('bank', 'zero'), may hold values from -0.0625 to 0.0625
- master_up: float32 [64, 2048, 1024], P('bank', 'zero'), may hold values from -0.1875 to 0.1875
- second_up: bfloat16 [64, 2048, 1024], P('bank', 'zero'), may hold values from -0.0625 to 0.0625
- master_down: float32 [64, 1024, 2048], P('bank', None, 'zero'), may hold values from -0.25 to 0.25
- second_down: bfloat16 [64, 1024, 2048], P('bank', None, 'zero'), may hold values from -0.09375 to 0.09375
- router_weight: float32 [2048, 64], P('zero', 'bank'), may hold values from -0.125 to 0.125
- router_gain: float32 [2048], P('zero'), may hold values from 0.25 to 1.75
Outputs:
- final_gate: bfloat16 [64, 2048, 1024], P('bank', None, 'zero')
- final_up: bfloat16 [64, 2048, 1024], P('bank', None, 'zero')
- final_down: bfloat16 [64, 1024, 2048], P('bank', 'zero')
- scale_gate: float32 [64, 1024], P('bank', 'zero')
- scale_up: float32 [64, 1024], P('bank', 'zero')
- scale_down: float32 [64, 1024], P('bank', 'zero')
- serve_router: bfloat16 [2048, 64], replicated
All inputs are finite; a program needn't handle non-finite values. Where the computation divides by a largest or mean magnitude, that divisor is 1e-20 or more.
Results may differ from a plain program's by a relative error of at most 0.001.
Values may be sent and summed in bfloat16 or wider, within the bound.
No kernel may reach another device: no remote copies, remote signals or barrier semaphores. Data moves between devices by JAX's collectives and lax.ppermute only.
A program may use at most 192 MiB of HBM per device.

v0:
```python
import jax
import jax.numpy as jnp
from jax import lax
from jax.sharding import PartitionSpec as P

D_MODEL = 2048


def on_device(
    master_gate,
    second_gate,
    master_up,
    second_up,
    master_down,
    second_down,
    router_weight,
    router_gain,
):
    merged_gate = master_gate + second_gate.astype(jnp.float32)
    merged_up = master_up + second_up.astype(jnp.float32)
    merged_down = master_down + second_down.astype(jnp.float32)
    total_gate, total_up, total_down = lax.psum(
        (
            jnp.sum(jnp.abs(merged_gate), axis=1),
            jnp.sum(jnp.abs(merged_up), axis=1),
            jnp.sum(jnp.abs(merged_down), axis=2),
        ),
        "zero",
    )
    scale_gate = total_gate / D_MODEL
    scale_up = total_up / D_MODEL
    scale_down = total_down / D_MODEL
    narrow_gate, narrow_up, narrow_down = (
        (merged_gate / jnp.expand_dims(scale_gate, 1)).astype(jnp.bfloat16),
        (merged_up / jnp.expand_dims(scale_up, 1)).astype(jnp.bfloat16),
        (merged_down / jnp.expand_dims(scale_down, 2)).astype(jnp.bfloat16),
    )
    final_gate, final_up = (
        lax.all_to_all(narrow_gate, "zero", split_axis=2, concat_axis=1, tiled=True),
        lax.all_to_all(narrow_up, "zero", split_axis=2, concat_axis=1, tiled=True),
    )
    final_down = lax.all_to_all(narrow_down, "zero", split_axis=1, concat_axis=2, tiled=True)
    scale_gate = lax.dynamic_slice_in_dim(
        scale_gate, lax.axis_index("zero") * final_gate.shape[2], final_gate.shape[2], axis=1
    )
    scale_up = lax.dynamic_slice_in_dim(
        scale_up, lax.axis_index("zero") * final_up.shape[2], final_up.shape[2], axis=1
    )
    scale_down = lax.dynamic_slice_in_dim(
        scale_down, lax.axis_index("zero") * final_down.shape[1], final_down.shape[1], axis=1
    )
    part_router = (router_weight * router_gain[:, None]).astype(jnp.bfloat16)
    row_router = lax.all_gather(part_router, "zero", axis=0, tiled=True)
    serve_router = lax.all_gather(row_router, "bank", axis=1, tiled=True)
    return (final_gate, final_up, final_down, scale_gate, scale_up, scale_down, serve_router)


def solution(mesh):
    return jax.shard_map(
        on_device,
        mesh=mesh,
        in_specs=(
            P("bank", "zero", None),
            P("bank", "zero", None),
            P("bank", "zero", None),
            P("bank", "zero", None),
            P("bank", None, "zero"),
            P("bank", None, "zero"),
            P("zero", "bank"),
            P("zero"),
        ),
        out_specs=(
            P("bank", None, "zero"),
            P("bank", None, "zero"),
            P("bank", "zero", None),
            P("bank", "zero"),
            P("bank", "zero"),
            P("bank", "zero"),
            P(),
        ),
        check_vma=False,
    )
```

profile of v0, /device:TPU:0, one launch (start us, length us, event | category | flops | bytes accessed | tf_op | source)
XLA Modules:
  0.0 554.7 jit_solution(10408405090956699153)
XLA Ops:
  7.2 0.0 all-reduce.3.cloned.1.call-start
  7.2 17.6 %copy.31 = f32[16,256,1024]{1,0,2:T(8,128)} copy(f32[16,256,1024]{2,1,0:T(8,128)} %param.8) | data formatting | bytes 33554432 | tf_op args[0]
  24.8 17.6 %copy.34 = f32[16,256,1024]{1,0,2:T(8,128)} copy(f32[16,256,1024]{2,1,0:T(8,128)} %param.10) | data formatting | bytes 33554432 | tf_op args[2]
  42.4 12.5 %copy.30 = bf16[16,256,1024]{1,0,2:T(8,128)(2,1)} copy(bf16[16,256,1024]{2,1,0:T(8,128)(2,1)} %param.9) | data formatting | bytes 16777216 | tf_op args[1]
  54.9 12.5 %copy.33 = bf16[16,256,1024]{1,0,2:T(8,128)(2,1)} copy(bf16[16,256,1024]{2,1,0:T(8,128)(2,1)} %param.11) | data formatting | bytes 16777216 | tf_op args[3]
  67.4 25.3 %abs_reduce_fusion = f32[16,1024]{0,1:T(8,128)} fusion(f32[16,1024,256]{2,1,0:T(8,128)} %param.12, bf16[16,1024,256]{2,1,0:T(8,128)(2,1)} %param.13), kind=kLoop, calls=%fused_computation.2 | loop fusion | flops 16760832 | bytes 25231360 | tf_op jit(solution)/shard_map/reduce_sum | solution.py:26
  92.7 0.0 copy-done
  92.7 0.0 copy-done.1
  92.7 13.2 %abs_reduce_fusion.1 = (f32[16,1024]{0,1:T(8,128)}, f32[16,1024]{0,1:T(8,128)}) fusion(f32[16,256,1024]{1,0,2:T(8,128)} %copy.34, bf16[16,256,1024]{1,0,2:T(8,128)(2,1)S(1)} %copy-done.1, f32[16,256,1024]{1,0,2:T(8,128)} %copy.31, bf16[16,256,1024]{1,0,2:T(8,128)(2,1)S(1)} %copy-done), kind=kLoop, calls=%fused_computation.4 | loop fusion | flops 33521664 | bytes 50462720 | tf_op jit(solution)/shard_map/reduce_sum | solution.py:25
  105.9 0.0 all-reduce.3.cloned.1.call-update
  105.9 62.0 %all-reduce.3.cloned.1.call-done = (f32[16,1024]{0,1:T(8,128)}, f32[16,1024]{0,1:T(8,128)}, f32[16,1024]{0,1:T(8,128)}) async-done(((f32[16,1024]{0,1:T(8,128)}, f32[16,1024]{0,1:T(8,128)}, f32[16,1024]{0,1:T(8,128)}), (f32[16,1024]{0,1:T(8,128)}, f32[16,1024]{0,1:T(8,128)}, f32[16,1024]{0,1:T(8,128)})) %all-reduce.3.cloned.1.call-update) | async-done | bytes 196624 | tf_op jit(solution)/shard_map/psum | solution.py:22
  167.9 1.1 broadcast_multiply_fusion.1
  169.0 12.0 %divide_convert_fusion.1 = bf16[16,256,1024]{1,0,2:T(8,128)(2,1)} fusion(f32[16,256,1024]{1,0,2:T(8,128)} %copy.34, bf16[16,256,1024]{1,0,2:T(8,128)(2,1)} %copy.33, f32[16,1024]{0,1:T(8,128)S(1)} %broadcast_multiply_fusion.1), kind=kLoop, calls=%fused_computation.3 | loop fusion | flops 16777216 | bytes 33619968 | tf_op jit(solution)/shard_map/convert_element_type | solution.py:35
  180.9 5.1 all-to-all-start.1
  186.0 0.0 copy-done.3
  186.1 12.0 %divide_convert_fusion.2 = bf16[16,256,1024]{1,0,2:T(8,128)(2,1)} fusion(f32[16,256,1024]{1,0,2:T(8,128)} %copy.31, bf16[16,256,1024]{1,0,2:T(8,128)(2,1)} %copy.30, f32[16,1024]{0,1:T(8,128)S(1)} %broadcast_multiply_fusion.2), kind=kLoop, calls=%fused_computation.6 | loop fusion | flops 16777216 | bytes 33619968 | tf_op jit(solution)/shard_map/convert_element_type | solution.py:34
  198.1 82.0 %all-to-all-done.1 = bf16[16,256,1024]{1,0,2:T(8,128)(2,1)} async-done(((bf16[16,256,1024]{1,0,2:T(8,128)(2,1)}), bf16[16,256,1024]{1,0,2:T(8,128)(2,1)}, u32[]{:S(2)}, u32[]{:S(2)}) %all-to-all-start.1) | async-done | bytes 8388640 | tf_op jit(solution)/shard_map/all_to_all | solution.py:40
  280.1 5.1 all-to-all-start
  285.3 23.8 %divide_convert_fusion = bf16[16,1024,256]{2,0,1:T(8,128)(2,1)} fusion(f32[16,1024,256]{2,1,0:T(8,128)} %param.12, f32[16,1024]{0,1:T(8,128)S(1)} %broadcast_multiply_fusion, bf16[16,1024,256]{2,1,0:T(8,128)(2,1)} %param.13), kind=kLoop, calls=%fused_computation.1 | loop fusion | flops 16777216 | bytes 33619968 | tf_op jit(solution)/shard_map/convert_element_type | solution.py:36
  309.0 70.0 %all-to-all-done = bf16[16,256,1024]{1,0,2:T(8,128)(2,1)} async-done(((bf16[16,256,1024]{1,0,2:T(8,128)(2,1)}), bf16[16,256,1024]{1,0,2:T(8,128)(2,1)}, u32[]{:S(2)}, u32[]{:S(2)}) %all-to-all-start) | async-done | bytes 8388640 | tf_op jit(solution)/shard_map/all_to_all | solution.py:39
  379.1 5.0 all-to-all-start.2
  384.1 97.2 %all_gather.6 = bf16[2048,16]{0,1:T(8,128)(2,1)S(1)} all-gather(bf16[256,16]{0,1:T(8,128)(2,1)S(1)} %multiply_convert_fusion), channel_id=1, replica_groups=mesh['bank'=4,'zero'=8] {'zero'}, dimensions={0}, use_global_device_ids=true | all-gather | bytes 73728 | tf_op jit(solution)/shard_map/all_gather | solution.py:53
  481.3 14.4 %all_gather.7 = bf16[2048,64]{0,1:T(8,128)(2,1)S(1)} all-gather(bf16[2048,16]{0,1:T(8,128)(2,1)S(1)} %all_gather.6), channel_id=1, replica_groups=mesh['bank'=4,'zero'=8] {'bank'}, dimensions={1}, use_global_device_ids=true | all-gather | bytes 327680 | tf_op jit(solution)/shard_map/all_gather | solution.py:54
  495.7 0.7 copy.39
  496.4 0.7 copy.40
  497.1 0.7 copy.41
  497.8 12.3 %copy.35 = bf16[16,8,256,128]{3,2,1,0:T(8,128)(2,1)} copy(bf16[16,8,256,128]{2,0,3,1:T(8,128)(2,1)} %bitcast.4) | data formatting | bytes 16777216 | tf_op jit(solution)/shard_map/all_to_all | solution.py:40
  510.0 12.3 %copy.32 = bf16[16,8,256,128]{3,2,1,0:T(8,128)(2,1)} copy(bf16[16,8,256,128]{2,0,3,1:T(8,128)(2,1)} %bitcast.1) | data formatting | bytes 16777216 | tf_op jit(solution)/shard_map/all_to_all | solution.py:39
  522.3 0.0 all-to-all-done.2
  522.3 11.4 %copy.38 = bf16[16,128,8,256]{3,2,1,0:T(8,128)(2,1)} copy(bf16[16,128,8,256]{3,0,1,2:T(8,128)(2,1)} %bitcast.7) | data formatting | bytes 16777216 | tf_op jit(solution)/shard_map/all_to_all | solution.py:42
  533.7 13.4 %all_to_all.50 = bf16[16,128,2048]{2,1,0:T(8,128)(2,1)} reshape(bf16[16,128,8,256]{3,2,1,0:T(8,128)(2,1)} %copy.38) | data formatting | bytes 16777216 | tf_op jit(solution)/shard_map/all_to_all | solution.py:42
  547.1 0.7 copy.53
  (15 shorter events, 0.1 us)
Async XLA Ops:
  7.2 160.7 %all-reduce.3.cloned.1.call-start = ((), (), s32[]{:S(2)}) async-start(), calls=%async_computation.3 | async-start | bytes 3145728 | tf_op jit(solution)/shard_map/psum | solution.py:22
  67.4 25.3 %copy-start = (bf16[16,256,1024]{1,0,2:T(8,128)(2,1)S(1)}, bf16[16,256,1024]{1,0,2:T(8,128)(2,1)}, u32[]{:S(2)}) copy-start(bf16[16,256,1024]{1,0,2:T(8,128)(2,1)} %copy.30) | copy-start | bytes 25165828
  67.4 25.3 %copy-start.1 = (bf16[16,256,1024]{1,0,2:T(8,128)(2,1)S(1)}, bf16[16,256,1024]{1,0,2:T(8,128)(2,1)}, u32[]{:S(2)}) copy-start(bf16[16,256,1024]{1,0,2:T(8,128)(2,1)} %copy.33) | copy-start | bytes 25165828
  180.9 5.1 copy-start.3
  180.9 99.1 %all-to-all-start.1 = ((bf16[16,256,1024]{1,0,2:T(8,128)(2,1)}), bf16[16,256,1024]{1,0,2:T(8,128)(2,1)}, u32[]{:S(2)}, u32[]{:S(2)}) async-start(bf16[16,256,1024]{1,0,2:T(8,128)(2,1)} %divide_convert_fusion.1), calls=%async_computation.1 | async-start | bytes 16777216 | tf_op jit(solution)/shard_map/all_to_all | solution.py:40
  198.1 87.1 %copy-start.2 = (f32[16,1024]{0,1:T(8,128)S(1)}, f32[16,1024]{0,1:T(8,128)}, u32[]{:S(2)}) copy-start(f32[16,1024]{0,1:T(8,128)} %get-tuple-element.16) | copy-start | bytes 196612
  280.1 99.0 %all-to-all-start = ((bf16[16,256,1024]{1,0,2:T(8,128)(2,1)}), bf16[16,256,1024]{1,0,2:T(8,128)(2,1)}, u32[]{:S(2)}, u32[]{:S(2)}) async-start(bf16[16,256,1024]{1,0,2:T(8,128)(2,1)} %divide_convert_fusion.2), calls=%async_computation | async-start | bytes 16777216 | tf_op jit(solution)/shard_map/all_to_all | solution.py:39
  309.0 75.1 %copy-start.4 = (f32[256,16]{0,1:T(8,128)S(1)}, f32[256,16]{0,1:T(8,128)}, u32[]{:S(2)}) copy-start(f32[256,16]{0,1:T(8,128)} %param.14) | copy-start | bytes 49156
  309.0 75.1 %copy-start.5 = (f32[256]{0:T(256)S(1)}, f32[256]{0:T(256)}, u32[]{:S(2)}) copy-start(f32[256]{0:T(256)} %param.15) | copy-start | bytes 3076
  379.1 143.3 %all-to-all-start.2 = ((bf16[16,1024,256]{2,0,1:T(8,128)(2,1)}), bf16[16,1024,256]{2,0,1:T(8,128)(2,1)}, u32[]{:S(2)}, u32[]{:S(2)}) async-start(bf16[16,1024,256]{2,0,1:T(8,128)(2,1)} %divide_convert_fusion), calls=%async_computation.2 | async-start | bytes 16777216 | tf_op jit(solution)/shard_map/all_to_all | solution.py:42
Sparse Core Ops, SparseCore 0:
  106.0 61.7 all-reduce.2
where the time goes:
time: 557 us; the launch traced here: 555 us
  waiting for transfers between devices  214 us (38%)
  local copies, waits for them, and re-layouts  112 us (20%)
  blocking collectives  112 us (20%)
  other arithmetic  87.4 us (16%)
  starting transfers between devices  15.3 us (3%)
  between operations  14.1 us (3%)
    all_gather x1, blocking collectives, on_device(): row_router = lax.all_gather(part_router, 'zero', axis=0, tiled=True)  97.2 us
    all_to_all x1, waiting for transfers between devices, on_device(): lax.all_to_all(narrow_up, 'zero', split_axis=2, concat_axis=1, tiled=True)  82 us
    all_to_all x1, waiting for transfers between devices, on_device(): lax.all_to_all(narrow_gate, 'zero', split_axis=2, concat_axis=1, tiled=True)  70 us
    unnamed x20, local copies, waits for them, and re-layouts  62.9 us
    psum x1, waiting for transfers between devices, on_device(): lax.psum((jnp.sum(jnp.abs(merged_gate), axis=1), jnp.sum(jnp.abs(merged_u...  62 us
    reduce_sum x1, other arithmetic, on_device(): jnp.sum(jnp.abs(merged_down), axis=2)  25.3 us
    all_to_all x2, local copies, waits for them, and re-layouts, on_device(): lax.all_to_all(narrow_down, 'zero', split_axis=1, concat_axis=2, tiled=True)  24.8 us
    convert_element_type x1, other arithmetic, on_device(): (merged_down / jnp.expand_dims(scale_down, 2)).astype(jnp.bfloat16)  23.8 us
  transfers between devices with their start and end apart: 4, of which 3 were waited for; matrix products, arithmetic and copies ran while one was open for 11% of the time, Pallas kernels for 0%

commit v1 on v0

--- a/solution.py
+++ b/solution.py
@@ -51,7 +51,7 @@
     )
     part_router = (router_weight * router_gain[:, None]).astype(jnp.bfloat16)
     row_router = lax.all_gather(part_router, "zero", axis=0, tiled=True)
-    serve_router = lax.all_gather(row_router, "bank", axis=1, tiled=True)
+    serve_router = jnp.concatenate(lax.all_gather(row_router, "bank"), axis=1)
     return (final_gate, final_up, final_down, scale_gate, scale_up, scale_down, serve_router)
 
 

time: 557 us -> 557 us (level)
    unnamed x20 -> x19, local copies, waits for them, and re-layouts: 62.9 us -> 62.2 us
where the time goes in v1:
time: 557 us; the launch traced here: 555 us
  waiting for transfers between devices  214 us (38%)
  local copies, waits for them, and re-layouts  112 us (20%)
  blocking collectives  112 us (20%)
  other arithmetic  87.4 us (16%)
  starting transfers between devices  15.3 us (3%)
  between operations  14.1 us (3%)
    all_gather x1, blocking collectives, on_device(): row_router = lax.all_gather(part_router, 'zero', axis=0, tiled=True)  97.2 us
    all_to_all x1, waiting for transfers between devices, on_device(): lax.all_to_all(narrow_up, 'zero', split_axis=2, concat_axis=1, tiled=True)  82 us
    all_to_all x1, waiting for transfers between devices, on_device(): lax.all_to_all(narrow_gate, 'zero', split_axis=2, concat_axis=1, tiled=True)  70 us
    unnamed x19, local copies, waits for them, and re-layouts  62.2 us
    psum x1, waiting for transfers between devices, on_device(): lax.psum((jnp.sum(jnp.abs(merged_gate), axis=1), jnp.sum(jnp.abs(merged_u...  62 us
    reduce_sum x1, other arithmetic, on_device(): jnp.sum(jnp.abs(merged_down), axis=2)  25.3 us
    all_to_all x2, local copies, waits for them, and re-layouts, on_device(): lax.all_to_all(narrow_down, 'zero', split_axis=1, concat_axis=2, tiled=True)  24.8 us
    convert_element_type x1, other arithmetic, on_device(): (merged_down / jnp.expand_dims(scale_down, 2)).astype(jnp.bfloat16)  23.8 us
  transfers between devices with their start and end apart: 4, of which 3 were waited for; matrix products, arithmetic and copies ran while one was open for 11% of the time, Pallas kernels for 0%

profile of v1, /device:TPU:0, one launch (start us, length us, event | category | flops | bytes accessed | tf_op | source)
XLA Modules:
  0.0 554.7 jit_solution(2122364816939443716)
XLA Ops:
  7.2 0.0 all-reduce.3.cloned.1.call-start
  7.2 17.6 %copy.33 = f32[16,256,1024]{1,0,2:T(8,128)} copy(f32[16,256,1024]{2,1,0:T(8,128)} %param.8) | data formatting | bytes 33554432 | tf_op args[0]
  24.8 17.6 %copy.36 = f32[16,256,1024]{1,0,2:T(8,128)} copy(f32[16,256,1024]{2,1,0:T(8,128)} %param.10) | data formatting | bytes 33554432 | tf_op args[2]
  42.4 12.5 %copy.32 = bf16[16,256,1024]{1,0,2:T(8,128)(2,1)} copy(bf16[16,256,1024]{2,1,0:T(8,128)(2,1)} %param.9) | data formatting | bytes 16777216 | tf_op args[1]
  54.9 12.5 %copy.35 = bf16[16,256,1024]{1,0,2:T(8,128)(2,1)} copy(bf16[16,256,1024]{2,1,0:T(8,128)(2,1)} %param.11) | data formatting | bytes 16777216 | tf_op args[3]
  67.4 25.3 %abs_reduce_fusion = f32[16,1024]{0,1:T(8,128)} fusion(f32[16,1024,256]{2,1,0:T(8,128)} %param.12, bf16[16,1024,256]{2,1,0:T(8,128)(2,1)} %param.13), kind=kLoop, calls=%fused_computation.2 | loop fusion | flops 16760832 | bytes 25231360 | tf_op jit(solution)/shard_map/reduce_sum | solution.py:26
  92.7 0.0 copy-done
  92.7 0.0 copy-done.1
  92.7 13.2 %abs_reduce_fusion.1 = (f32[16,1024]{0,1:T(8,128)}, f32[16,1024]{0,1:T(8,128)}) fusion(f32[16,256,1024]{1,0,2:T(8,128)} %copy.36, bf16[16,256,1024]{1,0,2:T(8,128)(2,1)S(1)} %copy-done.1, f32[16,256,1024]{1,0,2:T(8,128)} %copy.33, bf16[16,256,1024]{1,0,2:T(8,128)(2,1)S(1)} %copy-done), kind=kLoop, calls=%fused_computation.4 | loop fusion | flops 33521664 | bytes 50462720 | tf_op jit(solution)/shard_map/reduce_sum | solution.py:25
  105.9 0.0 all-reduce.3.cloned.1.call-update
  105.9 62.0 %all-reduce.3.cloned.1.call-done = (f32[16,1024]{0,1:T(8,128)}, f32[16,1024]{0,1:T(8,128)}, f32[16,1024]{0,1:T(8,128)}) async-done(((f32[16,1024]{0,1:T(8,128)}, f32[16,1024]{0,1:T(8,128)}, f32[16,1024]{0,1:T(8,128)}), (f32[16,1024]{0,1:T(8,128)}, f32[16,1024]{0,1:T(8,128)}, f32[16,1024]{0,1:T(8,128)})) %all-reduce.3.cloned.1.call-update) | async-done | bytes 196624 | tf_op jit(solution)/shard_map/psum | solution.py:22
  167.9 1.1 broadcast_multiply_fusion.1
  169.0 12.0 %divide_convert_fusion.1 = bf16[16,256,1024]{1,0,2:T(8,128)(2,1)} fusion(f32[16,256,1024]{1,0,2:T(8,128)} %copy.36, bf16[16,256,1024]{1,0,2:T(8,128)(2,1)} %copy.35, f32[16,1024]{0,1:T(8,128)S(1)} %broadcast_multiply_fusion.1), kind=kLoop, calls=%fused_computation.3 | loop fusion | flops 16777216 | bytes 33619968 | tf_op jit(solution)/shard_map/convert_element_type | solution.py:35
  180.9 5.1 all-to-all-start.1
  186.0 0.0 copy-done.3
  186.1 12.0 %divide_convert_fusion.2 = bf16[16,256,1024]{1,0,2:T(8,128)(2,1)} fusion(f32[16,256,1024]{1,0,2:T(8,128)} %copy.33, bf16[16,256,1024]{1,0,2:T(8,128)(2,1)} %copy.32, f32[16,1024]{0,1:T(8,128)S(1)} %broadcast_multiply_fusion.2), kind=kLoop, calls=%fused_computation.6 | loop fusion | flops 16777216 | bytes 33619968 | tf_op jit(solution)/shard_map/convert_element_type | solution.py:34
  198.1 82.0 %all-to-all-done.1 = bf16[16,256,1024]{1,0,2:T(8,128)(2,1)} async-done(((bf16[16,256,1024]{1,0,2:T(8,128)(2,1)}), bf16[16,256,1024]{1,0,2:T(8,128)(2,1)}, u32[]{:S(2)}, u32[]{:S(2)}) %all-to-all-start.1) | async-done | bytes 8388640 | tf_op jit(solution)/shard_map/all_to_all | solution.py:40
  280.1 5.1 all-to-all-start
  285.3 23.8 %divide_convert_fusion = bf16[16,1024,256]{2,0,1:T(8,128)(2,1)} fusion(f32[16,1024,256]{2,1,0:T(8,128)} %param.12, f32[16,1024]{0,1:T(8,128)S(1)} %broadcast_multiply_fusion, bf16[16,1024,256]{2,1,0:T(8,128)(2,1)} %param.13), kind=kLoop, calls=%fused_computation.1 | loop fusion | flops 16777216 | bytes 33619968 | tf_op jit(solution)/shard_map/convert_element_type | solution.py:36
  309.0 70.0 %all-to-all-done = bf16[16,256,1024]{1,0,2:T(8,128)(2,1)} async-done(((bf16[16,256,1024]{1,0,2:T(8,128)(2,1)}), bf16[16,256,1024]{1,0,2:T(8,128)(2,1)}, u32[]{:S(2)}, u32[]{:S(2)}) %all-to-all-start) | async-done | bytes 8388640 | tf_op jit(solution)/shard_map/all_to_all | solution.py:39
  379.1 5.0 all-to-all-start.2
  384.1 97.2 %all_gather.9 = bf16[2048,16]{0,1:T(8,128)(2,1)S(1)} all-gather(bf16[256,16]{0,1:T(8,128)(2,1)S(1)} %multiply_convert_fusion), channel_id=1, replica_groups=mesh['bank'=4,'zero'=8] {'zero'}, dimensions={0}, use_global_device_ids=true | all-gather | bytes 73728 | tf_op jit(solution)/shard_map/all_gather | solution.py:53
  481.3 14.4 %all-gather = bf16[8192,16]{0,1:T(8,128)(2,1)S(1)} all-gather(bf16[2048,16]{0,1:T(8,128)(2,1)S(1)} %all_gather.9), channel_id=2, replica_groups=mesh['bank'=4,'zero'=8] {'bank'}, dimensions={0}, use_global_device_ids=true | all-gather | bytes 327680 | tf_op jit(solution)/shard_map/all_gather | solution.py:54
  495.7 0.7 copy.54
  496.5 0.7 copy.42
  497.1 0.7 copy.43
  497.8 0.7 copy.44
  498.5 12.3 %copy.37 = bf16[16,8,256,128]{3,2,1,0:T(8,128)(2,1)} copy(bf16[16,8,256,128]{2,0,3,1:T(8,128)(2,1)} %bitcast.4) | data formatting | bytes 16777216 | tf_op jit(solution)/shard_map/all_to_all | solution.py:40
  510.8 12.3 %copy.34 = bf16[16,8,256,128]{3,2,1,0:T(8,128)(2,1)} copy(bf16[16,8,256,128]{2,0,3,1:T(8,128)(2,1)} %bitcast.1) | data formatting | bytes 16777216 | tf_op jit(solution)/shard_map/all_to_all | solution.py:39
  523.0 0.0 all-to-all-done.2
  523.0 11.4 %copy.40 = bf16[16,128,8,256]{3,2,1,0:T(8,128)(2,1)} copy(bf16[16,128,8,256]{3,0,1,2:T(8,128)(2,1)} %bitcast.7) | data formatting | bytes 16777216 | tf_op jit(solution)/shard_map/all_to_all | solution.py:42
  534.4 13.4 %all_to_all.50 = bf16[16,128,2048]{2,1,0:T(8,128)(2,1)} reshape(bf16[16,128,8,256]{3,2,1,0:T(8,128)(2,1)} %copy.40) | data formatting | bytes 16777216 | tf_op jit(solution)/shard_map/all_to_all | solution.py:42
  (15 shorter events, 0.1 us)
Async XLA Ops:
  7.2 160.7 %all-reduce.3.cloned.1.call-start = ((), (), s32[]{:S(2)}) async-start(), calls=%async_computation.3 | async-start | bytes 3145728 | tf_op jit(solution)/shard_map/psum | solution.py:22
  67.4 25.3 %copy-start = (bf16[16,256,1024]{1,0,2:T(8,128)(2,1)S(1)}, bf16[16,256,1024]{1,0,2:T(8,128)(2,1)}, u32[]{:S(2)}) copy-start(bf16[16,256,1024]{1,0,2:T(8,128)(2,1)} %copy.32) | copy-start | bytes 25165828
  67.4 25.3 %copy-start.1 = (bf16[16,256,1024]{1,0,2:T(8,128)(2,1)S(1)}, bf16[16,256,1024]{1,0,2:T(8,128)(2,1)}, u32[]{:S(2)}) copy-start(bf16[16,256,1024]{1,0,2:T(8,128)(2,1)} %copy.35) | copy-start | bytes 25165828
  180.9 5.1 copy-start.3
  180.9 99.1 %all-to-all-start.1 = ((bf16[16,256,1024]{1,0,2:T(8,128)(2,1)}), bf16[16,256,1024]{1,0,2:T(8,128)(2,1)}, u32[]{:S(2)}, u32[]{:S(2)}) async-start(bf16[16,256,1024]{1,0,2:T(8,128)(2,1)} %divide_convert_fusion.1), calls=%async_computation.1 | async-start | bytes 16777216 | tf_op jit(solution)/shard_map/all_to_all | solution.py:40
  198.1 87.1 %copy-start.2 = (f32[16,1024]{0,1:T(8,128)S(1)}, f32[16,1024]{0,1:T(8,128)}, u32[]{:S(2)}) copy-start(f32[16,1024]{0,1:T(8,128)} %get-tuple-element.16) | copy-start | bytes 196612
  280.1 99.0 %all-to-all-start = ((bf16[16,256,1024]{1,0,2:T(8,128)(2,1)}), bf16[16,256,1024]{1,0,2:T(8,128)(2,1)}, u32[]{:S(2)}, u32[]{:S(2)}) async-start(bf16[16,256,1024]{1,0,2:T(8,128)(2,1)} %divide_convert_fusion.2), calls=%async_computation | async-start | bytes 16777216 | tf_op jit(solution)/shard_map/all_to_all | solution.py:39
  309.0 75.1 %copy-start.4 = (f32[256,16]{0,1:T(8,128)S(1)}, f32[256,16]{0,1:T(8,128)}, u32[]{:S(2)}) copy-start(f32[256,16]{0,1:T(8,128)} %param.14) | copy-start | bytes 49156
  309.0 75.1 %copy-start.5 = (f32[256]{0:T(256)S(1)}, f32[256]{0:T(256)}, u32[]{:S(2)}) copy-start(f32[256]{0:T(256)} %param.15) | copy-start | bytes 3076
  379.1 144.0 %all-to-all-start.2 = ((bf16[16,1024,256]{2,0,1:T(8,128)(2,1)}), bf16[16,1024,256]{2,0,1:T(8,128)(2,1)}, u32[]{:S(2)}, u32[]{:S(2)}) async-start(bf16[16,1024,256]{2,0,1:T(8,128)(2,1)} %divide_convert_fusion), calls=%async_computation.2 | async-start | bytes 16777216 | tf_op jit(solution)/shard_map/all_to_all | solution.py:42
Sparse Core Ops, SparseCore 0:
  106.0 61.7 all-reduce.2
